TPU v7x, 32 devices: a whole 2x2x4 slice. The times are simulated.
32 devices in a mesh: grp: 4 (over y, core), rep: 8 (over z, x).
Axes of the slice: x: 2, y: 2, z: 4, core: 2. Of those that a mesh axis runs over, the one named last changes fastest.
Arguments:
- coefficients: bfloat16 [4096, 2048], P(('grp', 'rep')), may hold values from -100 to 100
- truncation: int32 [16], replicated, may hold values from 16 to 64
- neighbours: int32 [50, 4096], P(None, ('grp', 'rep')), may hold values from 0 to 4095, as said below
- initial: float32 [32, 4096], P(None, ('grp', 'rep')), may hold values from -6 to 6
Outputs:
- alignment: float32 [2, 50, 4096], P(None, None, ('grp', 'rep'))
- vectors: float32 [32, 4096], P(None, ('grp', 'rep'))
Inputs may be any that keep to these rules, and one draw needn't show every extreme that they name: `neighbours`: every neighbour of a particle is another particle of the same block of 1024 particles that holds it (the particles of one group of 8 devices along rep). For each device, the neighbour slots of its 128 particles that name particles of one other device number at most 64; every device has, in every draw, one other device that its slots name exactly 64 times.
All inputs are finite; a program needn't handle non-finite values.
Results may differ from a plain program's by a relative error of at most 0.0003.
Values may be sent and summed in bfloat16 or wider, within the bound.
A program may use at most 128 MiB of HBM per device.

v0:
```python
import math

import jax
import jax.numpy as jnp
from jax import lax
from jax.sharding import PartitionSpec as P

ANG = 64
RAD = 16
ANGLES = 256
NB = 50
ITERS = 3


epsilon = 1e-06


def rotation_angle_grid(angular, samples):
    frequency = jnp.arange(angular, dtype=jnp.float32)
    sample_angle = jnp.arange(samples, dtype=jnp.float32) * (2.0 * math.pi / samples)
    phases = frequency[:, None] * sample_angle[None, :]
    transform = jnp.concatenate([jnp.cos(phases), -jnp.sin(phases)], axis=0)
    return (transform, jnp.cos(sample_angle), jnp.sin(sample_angle))


def kept_mask(truncation):
    levels = jnp.arange(ANG, dtype=jnp.int32)
    return (levels[None, :] < truncation[:, None]).astype(jnp.float32)


def pair_moments(own_rows, other_rows, weights, transform, cosine_row, sine_row):
    row_count = own_rows.shape[0]
    masked = own_rows.astype(jnp.float32).reshape(row_count, 2, RAD, ANG) * weights
    partner = other_rows.reshape(NB, row_count, 2, RAD, ANG).astype(jnp.float32)
    own_real = masked[None, :, 0]
    own_imag = masked[None, :, 1]
    partner_real = partner[:, :, 0]
    partner_imag = partner[:, :, 1]
    real_fourier_coeffs = jnp.sum(own_real * partner_real + own_imag * partner_imag, axis=2)
    imaginary_fourier_coeffs = jnp.sum(own_imag * partner_real - own_real * partner_imag, axis=2)
    spectrum = jnp.concatenate([real_fourier_coeffs, imaginary_fourier_coeffs], axis=2)
    correlation = jnp.einsum("nbk,km->nbm", spectrum, transform, precision=lax.Precision.HIGHEST)
    squared = correlation * correlation
    energy = jnp.mean(squared, axis=2)
    moment_real = jnp.mean(squared * cosine_row, axis=2)
    moment_imaginary = jnp.mean(squared * sine_row, axis=2)
    return (energy, moment_real, moment_imaginary)


def lower_inverse(lower):
    matrix_order = lower.shape[0]
    identity = jnp.eye(matrix_order, dtype=lower.dtype)
    inverse_rows = []
    for target in range(matrix_order):
        running = identity[target]
        for source in range(target):
            running = running - lower[target, source] * inverse_rows[source]
        inverse_rows.append(running / lower[target, target])
    return jnp.stack(inverse_rows)


def shards(coefficients, truncation, neighbours, initial):
    maximum_frequency = lax.Precision.HIGHEST
    groups = lax.axis_size("grp")
    replicas = lax.axis_size("rep")
    particles = coefficients.shape[0]
    particle_total = particles * groups * replicas
    group_start = lax.axis_index("grp") * (replicas * particles)
    in_group = neighbours - group_start
    weights = kept_mask(truncation)
    transform, cosine_row, sine_row = rotation_angle_grid(ANG, ANGLES)
    rows_all = lax.all_gather(coefficients, "rep", axis=0, tiled=True)
    block_width = math.gcd(particles, 32)
    blocks = particles // block_width
    own_blocks = coefficients.reshape(blocks, block_width, coefficients.shape[1])
    index_blocks = in_group.reshape(NB, blocks, block_width).transpose(1, 0, 2)

    def one_block(operands):
        own_rows, indices = operands
        other_rows = jnp.take(rows_all, indices.reshape(-1), axis=0)
        return pair_moments(own_rows, other_rows, weights, transform, cosine_row, sine_row)

    energy, moment_real, moment_imaginary = lax.map(one_block, (own_blocks, index_blocks))
    energy = energy.transpose(1, 0, 2).reshape(NB, particles)
    moment_real = moment_real.transpose(1, 0, 2).reshape(NB, particles)
    moment_imaginary = moment_imaginary.transpose(1, 0, 2).reshape(NB, particles)
    alignment = jnp.stack([moment_real / (energy + epsilon), moment_imaginary / (energy + epsilon)])
    degree = epsilon + jnp.sum(energy, axis=0)
    vector_count = initial.shape[0] // 2
    current = initial
    factor = jnp.eye(vector_count, dtype=jnp.float32)
    for iteration in range(ITERS):
        whole = lax.all_gather(current, "rep", axis=1, tiled=True)
        picked = jnp.take(whole, in_group.reshape(-1), axis=1).reshape(
            current.shape[0], NB, particles
        )
        real_part = picked[:vector_count]
        imag_part = picked[vector_count:]
        apply_image_real = (
            jnp.sum(moment_real * real_part - moment_imaginary * imag_part, axis=1) / degree
        )
        apply_image_imag = (
            jnp.sum(moment_real * imag_part + moment_imaginary * real_part, axis=1) / degree
        )
        raw_matrix = lax.psum(
            (
                jnp.dot(apply_image_real, apply_image_real.T, precision=maximum_frequency)
                + jnp.dot(apply_image_imag, apply_image_imag.T, precision=maximum_frequency)
            )
            / particle_total,
            ("grp", "rep"),
        )
        folded = jnp.dot(
            jnp.dot(factor, raw_matrix, precision=maximum_frequency),
            factor.T,
            precision=maximum_frequency,
        )
        factor = jnp.dot(
            lower_inverse(jnp.linalg.cholesky(folded)), factor, precision=maximum_frequency
        )
        current = jnp.concatenate([apply_image_real, apply_image_imag], axis=0)
    vectors = jnp.concatenate(
        [
            jnp.dot(factor, current[:vector_count], precision=maximum_frequency),
            jnp.dot(factor, current[vector_count:], precision=maximum_frequency),
        ],
        axis=0,
    )
    return (alignment, vectors)


def solution(mesh):
    in_specs = (P(("grp", "rep"), None), P(), P(None, ("grp", "rep")), P(None, ("grp", "rep")))
    out_specs = (P(None, None, ("grp", "rep")), P(None, ("grp", "rep")))
    return jax.shard_map(shards, mesh=mesh, in_specs=in_specs, out_specs=out_specs, check_vma=False)
```

profile of v0, /device:TPU:0, one launch (start us, length us, event | category | flops | bytes accessed | tf_op | source)
XLA Modules:
  0.0 799.1 jit_solution(13136473731412117588)
XLA Ops:
  9.6 35.1 %all_gather.13 = f32[32,1024]{0,1:T(8,128)S(1)} all-gather(f32[32,128]{0,1:T(8,128)S(1)} %copy.107), channel_id=1, replica_groups=mesh['grp'=4,'rep'=8] {'rep'}, dimensions={1}, use_global_device_ids=true | all-gather | bytes 147456 | tf_op jit(solution)/shard_map/all_gather | solution.py:93
  44.8 12.6 %gather_fusion.1 = f32[6400,32]{1,0:T(8,128)} fusion(f32[32,1024]{0,1:T(8,128)S(1)} %all_gather.13, s32[7168]{0:T(1024)S(1)} %pad_clamp_fusion.1), kind=kCustom, calls=%fused_computation.1.clone | custom fusion | bytes 1664000 | tf_op jit(solution)/shard_map/jit(_take)/gather | solution.py:94
  58.3 5.3 select_bitcast_fusion.2
  67.2 21.3 %all-gather.2.cloned.1.call-done = bf16[1024,2048]{1,0:T(8,128)(2,1)} async-done(((bf16[128,2048]{1,0:T(8,128)(2,1)}), bf16[1024,2048]{1,0:T(8,128)(2,1)}) %all-gather.2.cloned.1.call-update) | async-done | bytes 4194320 | tf_op jit(solution)/shard_map/all_gather | solution.py:72
  88.5 269.3 %while.15 = (s32[]{:T(128)}, f32[4,50,32]{2,1,0:T(8,128)S(1)}, f32[4,50,32]{2,1,0:T(8,128)S(1)}, f32[4,50,32]{2,1,0:T(8,128)S(1)}, bf16[4,32,2048]{2,1,0:T(8,128...) while((s32[]{:T(128)}, f32[4,50,32]{2,1,0:T(8,128)S(1)}, ...), condition=%wide.region_6.7_spmd.clone, body=%wide.region_0.6_spmd.clone.sunk | while | flops 651414080 | bytes 63265588 | solution.py:83
  88.8 17.0 %gather_fusion = bf16[1600,2048]{1,0:T(8,128)(2,1)} fusion(bf16[1024,2048]{1,0:T(8,128)(2,1)} %get-tuple-element.755, s32[2048]{0:T(1024)S(1)} %pad_clamp_fusion.3), kind=kCustom, calls=%fused_computation.clone.clone.1 | custom fusion | bytes 13113600 | tf_op jit(solution)/shard_map/while/body/eval_jaxpr/jit(_take)/gather | solution.py:80
  105.8 19.3 %gather.27 = bf16[50,32,2,16,64]{4,3,2,1,0:T(8,128)(2,1)} reshape(bf16[1600,2048]{1,0:T(8,128)(2,1)} %gather_fusion) | data formatting | bytes 13107200 | tf_op jit(solution)/shard_map/while/body/eval_jaxpr/jit(_take)/gather | solution.py:80
  125.1 14.8 %select_convert_fusion.2 = f32[50,32,2,16,64]{4,3,2,1,0:T(8,128)} fusion(bf16[50,32,2,16,64]{4,3,2,1,0:T(8,128)(2,1)} %gather.27, pred[50,32]{1,0:T(8,128)(4,1)S(1)} %compare_and_fusion.3), kind=kLoop, calls=%fused_computation.11.clone.1 | loop fusion | flops 6553600 | bytes 19662400 | tf_op jit(solution)/shard_map/while/body/eval_jaxpr/convert_element_type | solution.py:34
  141.2 12.6 %add_reduce_fusion.5 = (f32[50,32,64]{2,1,0:T(8,128)S(1)}, f32[50,32,64]{2,1,0:T(8,128)S(1)}) fusion(f32[50,32,2,16,64]{4,3,2,1,0:T(8,128)} %select_convert_fusion.2, f32[32,16,64]{2,1,0:T(8,128)S(1)} %get-tuple-element.720, f32[32,16,64]{2,1,0:T(8,128)S(1)} %get-tuple-element.721), kind=kLoop, calls=%fused_computation.10.clone.1 | loop fusion | flops 12902400 | bytes 14188544 | tf_op jit(solution)/shard_map/while/body/eval_jaxpr/reduce_sum | solution.py:39
  156.1 17.0 %gather_fusion = bf16[1600,2048]{1,0:T(8,128)(2,1)} fusion(bf16[1024,2048]{1,0:T(8,128)(2,1)} %get-tuple-element.755, s32[2048]{0:T(1024)S(1)} %pad_clamp_fusion.3), kind=kCustom, calls=%fused_computation.clone.clone.1 | custom fusion | bytes 13113600 | tf_op jit(solution)/shard_map/while/body/eval_jaxpr/jit(_take)/gather | solution.py:80
  173.1 19.3 %gather.27 = bf16[50,32,2,16,64]{4,3,2,1,0:T(8,128)(2,1)} reshape(bf16[1600,2048]{1,0:T(8,128)(2,1)} %gather_fusion) | data formatting | bytes 13107200 | tf_op jit(solution)/shard_map/while/body/eval_jaxpr/jit(_take)/gather | solution.py:80
  192.4 14.8 %select_convert_fusion.2 = f32[50,32,2,16,64]{4,3,2,1,0:T(8,128)} fusion(bf16[50,32,2,16,64]{4,3,2,1,0:T(8,128)(2,1)} %gather.27, pred[50,32]{1,0:T(8,128)(4,1)S(1)} %compare_and_fusion.3), kind=kLoop, calls=%fused_computation.11.clone.1 | loop fusion | flops 6553600 | bytes 19662400 | tf_op jit(solution)/shard_map/while/body/eval_jaxpr/convert_element_type | solution.py:34
  208.5 12.6 %add_reduce_fusion.5 = (f32[50,32,64]{2,1,0:T(8,128)S(1)}, f32[50,32,64]{2,1,0:T(8,128)S(1)}) fusion(f32[50,32,2,16,64]{4,3,2,1,0:T(8,128)} %select_convert_fusion.2, f32[32,16,64]{2,1,0:T(8,128)S(1)} %get-tuple-element.720, f32[32,16,64]{2,1,0:T(8,128)S(1)} %get-tuple-element.721), kind=kLoop, calls=%fused_computation.10.clone.1 | loop fusion | flops 12902400 | bytes 14188544 | tf_op jit(solution)/shard_map/while/body/eval_jaxpr/reduce_sum | solution.py:39
  223.4 17.0 %gather_fusion = bf16[1600,2048]{1,0:T(8,128)(2,1)} fusion(bf16[1024,2048]{1,0:T(8,128)(2,1)} %get-tuple-element.755, s32[2048]{0:T(1024)S(1)} %pad_clamp_fusion.3), kind=kCustom, calls=%fused_computation.clone.clone.1 | custom fusion | bytes 13113600 | tf_op jit(solution)/shard_map/while/body/eval_jaxpr/jit(_take)/gather | solution.py:80
  240.5 19.3 %gather.27 = bf16[50,32,2,16,64]{4,3,2,1,0:T(8,128)(2,1)} reshape(bf16[1600,2048]{1,0:T(8,128)(2,1)} %gather_fusion) | data formatting | bytes 13107200 | tf_op jit(solution)/shard_map/while/body/eval_jaxpr/jit(_take)/gather | solution.py:80
  259.7 14.8 %select_convert_fusion.2 = f32[50,32,2,16,64]{4,3,2,1,0:T(8,128)} fusion(bf16[50,32,2,16,64]{4,3,2,1,0:T(8,128)(2,1)} %gather.27, pred[50,32]{1,0:T(8,128)(4,1)S(1)} %compare_and_fusion.3), kind=kLoop, calls=%fused_computation.11.clone.1 | loop fusion | flops 6553600 | bytes 19662400 | tf_op jit(solution)/shard_map/while/body/eval_jaxpr/convert_element_type | solution.py:34
  275.8 12.6 %add_reduce_fusion.5 = (f32[50,32,64]{2,1,0:T(8,128)S(1)}, f32[50,32,64]{2,1,0:T(8,128)S(1)}) fusion(f32[50,32,2,16,64]{4,3,2,1,0:T(8,128)} %select_convert_fusion.2, f32[32,16,64]{2,1,0:T(8,128)S(1)} %get-tuple-element.720, f32[32,16,64]{2,1,0:T(8,128)S(1)} %get-tuple-element.721), kind=kLoop, calls=%fused_computation.10.clone.1 | loop fusion | flops 12902400 | bytes 14188544 | tf_op jit(solution)/shard_map/while/body/eval_jaxpr/reduce_sum | solution.py:39
  290.8 17.0 %gather_fusion = bf16[1600,2048]{1,0:T(8,128)(2,1)} fusion(bf16[1024,2048]{1,0:T(8,128)(2,1)} %get-tuple-element.755, s32[2048]{0:T(1024)S(1)} %pad_clamp_fusion.3), kind=kCustom, calls=%fused_computation.clone.clone.1 | custom fusion | bytes 13113600 | tf_op jit(solution)/shard_map/while/body/eval_jaxpr/jit(_take)/gather | solution.py:80
  307.8 19.3 %gather.27 = bf16[50,32,2,16,64]{4,3,2,1,0:T(8,128)(2,1)} reshape(bf16[1600,2048]{1,0:T(8,128)(2,1)} %gather_fusion) | data formatting | bytes 13107200 | tf_op jit(solution)/shard_map/while/body/eval_jaxpr/jit(_take)/gather | solution.py:80
  327.1 14.8 %select_convert_fusion.2 = f32[50,32,2,16,64]{4,3,2,1,0:T(8,128)} fusion(bf16[50,32,2,16,64]{4,3,2,1,0:T(8,128)(2,1)} %gather.27, pred[50,32]{1,0:T(8,128)(4,1)S(1)} %compare_and_fusion.3), kind=kLoop, calls=%fused_computation.11.clone.1 | loop fusion | flops 6553600 | bytes 19662400 | tf_op jit(solution)/shard_map/while/body/eval_jaxpr/convert_element_type | solution.py:34
  343.2 12.6 %add_reduce_fusion.5 = (f32[50,32,64]{2,1,0:T(8,128)S(1)}, f32[50,32,64]{2,1,0:T(8,128)S(1)}) fusion(f32[50,32,2,16,64]{4,3,2,1,0:T(8,128)} %select_convert_fusion.2, f32[32,16,64]{2,1,0:T(8,128)S(1)} %get-tuple-element.720, f32[32,16,64]{2,1,0:T(8,128)S(1)} %get-tuple-element.721), kind=kLoop, calls=%fused_computation.10.clone.1 | loop fusion | flops 12902400 | bytes 14188544 | tf_op jit(solution)/shard_map/while/body/eval_jaxpr/reduce_sum | solution.py:39
  358.4 4.9 add_reduce_fusion.3
  363.8 31.8 %all_gather.14 = f32[32,1024]{0,1:T(8,128)S(1)} all-gather(f32[32,128]{0,1:T(8,128)S(1)} %pad_maximum_fusion.1), channel_id=1, replica_groups=mesh['grp'=4,'rep'=8] {'rep'}, dimensions={1}, use_global_device_ids=true | all-gather | bytes 147456 | tf_op jit(solution)/shard_map/all_gather | solution.py:93
  395.5 12.6 %gather_fusion.2 = f32[6400,32]{1,0:T(8,128)} fusion(f32[32,1024]{0,1:T(8,128)S(1)} %all_gather.14, s32[7168]{0:T(1024)S(1)} %copy-done.1), kind=kCustom, calls=%fused_computation.2.clone | custom fusion | bytes 1664000 | tf_op jit(solution)/shard_map/jit(_take)/gather | solution.py:94
  408.1 5.2 select_bitcast_fusion.1
  417.0 31.5 %all_gather.15 = f32[32,1024]{0,1:T(8,128)S(1)} all-gather(f32[32,128]{0,1:T(8,128)S(1)} %pad_maximum_fusion.2), channel_id=1, replica_groups=mesh['grp'=4,'rep'=8] {'rep'}, dimensions={1}, use_global_device_ids=true | all-gather | bytes 147456 | tf_op jit(solution)/shard_map/all_gather | solution.py:93
  448.5 12.6 %gather_fusion.3 = f32[6400,32]{1,0:T(8,128)} fusion(f32[32,1024]{0,1:T(8,128)S(1)} %all_gather.15, s32[7168]{0:T(1024)S(1)} %copy-done.1), kind=kCustom, calls=%fused_computation.3.clone | custom fusion | bytes 1664000 | tf_op jit(solution)/shard_map/jit(_take)/gather | solution.py:94
  461.1 5.2 select_bitcast_fusion
  470.7 37.3 %all-reduce = (f32[16,16]{1,0:T(8,128)S(1)}, f32[16,16]{1,0:T(8,128)S(1)}, f32[16,16]{1,0:T(8,128)S(1)}) all-reduce(f32[16,16]{1,0:T(8,128)S(1)} %fusion.17, f32[16,16]{1,0:T(8,128)S(1)} %fusion.16, f32[16,16]{1,0:T(8,128)S(1)} %fusion.15), channel_id=1, replica_groups=mesh['grp'=4,'rep'=8] {'grp','rep'}, use_global_device_ids=true, to_apply=%region_10.12 | all-reduce | flops 768 | bytes 6144 | tf_op jit(solution)/shard_map/psum | solution.py:105
  516.9 84.9 %subtract_divide_fusion.30 = (f32[1,16]{1,0:T(1,128)S(1)}, f32[1,16]{1,0:T(1,128)S(1)}, f32[1,16]{1,0:T(1,128)S(1)}, f32[1,16]{1,0:T(1,128)S(1)}, f32[1,16]{1,0:...) fusion(f32[]{:T(128)} %bitcast.150, ...), kind=kLoop, calls=%fused_computation.131 | loop fusion | flops 4096 | bytes 2592 | tf_op jit(solution)/shard_map/div | solution.py:58
  610.8 84.9 %subtract_divide_fusion.15 = (f32[1,16]{1,0:T(1,128)S(1)}, f32[1,16]{1,0:T(1,128)S(1)}, f32[1,16]{1,0:T(1,128)S(1)}, f32[1,16]{1,0:T(1,128)S(1)}, f32[1,16]{1,0:...) fusion(f32[]{:T(128)} %bitcast.290, ...), kind=kLoop, calls=%fused_computation.116 | loop fusion | flops 4096 | bytes 2592 | tf_op jit(solution)/shard_map/div | solution.py:58
  704.8 84.9 %subtract_divide_fusion = (f32[1,16]{1,0:T(1,128)S(1)}, f32[1,16]{1,0:T(1,128)S(1)}, f32[1,16]{1,0:T(1,128)S(1)}, f32[1,16]{1,0:T(1,128)S(1)}, f32[1,16]{1,0:T(1...) fusion(f32[]{:T(128)} %bitcast.430, ...), kind=kLoop, calls=%fused_computation.101 | loop fusion | flops 4096 | bytes 2592 | tf_op jit(solution)/shard_map/div | solution.py:58
  (174 shorter events, 59.3 us)
Async XLA Ops:
  7.2 81.4 %all-gather.2.cloned.1.call-start = ((), (), s32[]{:S(2)}) async-start(), calls=%async_computation | async-start | bytes 4718592 | tf_op jit(solution)/shard_map/all_gather | solution.py:72
  8.7 49.5 %copy-start.3 = (pred[6400]{0:T(1024)(128)(4,1)}, pred[6400]{0:T(1024)(128)(4,1)S(1)}, u32[]{:S(2)}) copy-start(pred[6400]{0:T(1024)(128)(4,1)S(1)} %get-tuple-element.227) | copy-start | bytes 19204
  44.7 12.6 %copy-start = (s32[7168]{0:T(1024)}, s32[7168]{0:T(1024)S(1)}, u32[]{:S(2)}) copy-start(s32[7168]{0:T(1024)S(1)} %pad_clamp_fusion.1) | copy-start | bytes 86020
  63.5 25.0 %copy-start.5 = (s32[16]{0:T(128)S(1)}, s32[16]{0:T(128)}, u32[]{:S(2)}) copy-start(s32[16]{0:T(128)} %param.10) | copy-start | bytes 196
  358.4 37.2 %copy-start.1 = (s32[7168]{0:T(1024)S(1)}, s32[7168]{0:T(1024)}, u32[]{:S(2)}) copy-start(s32[7168]{0:T(1024)} %copy-done) | copy-start | bytes 86020
  395.5 12.6 %copy-start.4 = (pred[6400]{0:T(1024)(128)(4,1)S(1)}, pred[6400]{0:T(1024)(128)(4,1)}, u32[]{:S(2)}) copy-start(pred[6400]{0:T(1024)(128)(4,1)} %copy-done.3) | copy-start | bytes 19204
  467.4 49.5 %copy-start.2 = (f32[16,16]{1,0:T(8,128)S(1)}, f32[16,16]{1,0:T(8,128)}, u32[]{:S(2)}) copy-start(f32[16,16]{1,0:T(8,128)} %fusion.32) | copy-start | bytes 3076
Sparse Core Ops, SparseCore 0:
  10.1 78.3 all-gather.1
where the time goes:
time: 807 us; the launch traced here: 799 us
  other arithmetic  406 us (50%)
  local copies, waits for them, and re-layouts  210 us (26%)
  blocking collectives  136 us (17%)
  waiting for transfers between devices  22 us (3%)
  between operations  14.4 us (2%)
  matrix products  10.8 us (1%)
    div x3, other arithmetic, lower_inverse(): inverse_rows.append(running / lower[target, target])  255 us
    gather x8, local copies, waits for them, and re-layouts, one_block(): other_rows = jnp.take(rows_all, indices.reshape(-1), axis=0)  145 us
    all_gather x3, blocking collectives, shards(): whole = lax.all_gather(current, 'rep', axis=1, tiled=True)  98.3 us
    convert_element_type x4, other arithmetic, pair_moments(): partner = other_rows.reshape(NB, row_count, 2, RAD, ANG).astype(jnp.float32)  59.1 us
    reduce_sum x4, other arithmetic, pair_moments(): jnp.sum(own_real * partner_real + own_imag * partner_imag, axis=2)  50.6 us
    gather x3, local copies, waits for them, and re-layouts, shards(): jnp.take(whole, in_group.reshape(-1), axis=1)  37.8 us
    psum x1, blocking collectives, shards(): lax.psum((jnp.dot(apply_image_real, apply_image_real.T, precision=maximum...  37.3 us
    all_gather x1, waiting for transfers between devices, shards(): rows_all = lax.all_gather(coefficients, 'rep', axis=0, tiled=True)  21.3 us
  transfers between devices with their start and end apart: 1, of which 1 were waited for; matrix products, arithmetic and copies ran while one was open for 3% of the time, Pallas kernels for 0%

commit v1 on v0

v1 whole, which is shorter than its diff:
```python
import functools
import math

import jax
import jax.numpy as jnp
from jax import lax
from jax.experimental import pallas as pl
from jax.experimental.pallas import tpu as pltpu
from jax.sharding import PartitionSpec as P

ANG = 64
RAD = 16
ITERS = 3
EPS = 1e-06
VMEM = pl.BlockSpec(memory_space=pltpu.VMEM)


def moments_kernel(own_ref, all_ref, slots_ref, slots_t_ref, align_ref, oper_ref, degree_ref, ar_ref, ai_ref):
    blocks, _, _, wide = all_ref.shape
    own = own_ref.shape[2] // 2
    slots = slots_ref.shape[0]
    half = wide // 2

    degree_ref[...] = jnp.full(degree_ref.shape, EPS, jnp.float32)

    def tile(step, _):
        block = step // 2
        part = step % 2
        energy = moment_re = moment_im = before_re = before_im = None
        for k in range(ANG):
            partner = all_ref[block, k].T
            partner = jnp.where(part == 0, partner[:half], partner[half:])
            spectrum = jnp.dot(partner, own_ref[k], preferred_element_type=jnp.float32)
            re, im = spectrum[:, :own], spectrum[:, own:]
            if k == 0:
                energy = 2.0 * (re * re)
                before_re = 2.0 * re
                continue
            energy = energy + (re * re + im * im)
            if k == 1:
                moment_re = before_re * re
                moment_im = -(before_re * im)
            else:
                moment_re = moment_re + (before_re * re + before_im * im)
                moment_im = moment_im + (before_im * re - before_re * im)
            before_re, before_im = re, im
        energy, moment_re, moment_im = 0.5 * energy, 0.5 * moment_re, 0.5 * moment_im
        first = pl.multiple_of(step * half, half)
        rows = pl.ds(first, half)
        name = lax.broadcasted_iota(jnp.int32, (half, own), 0) + first
        count = jnp.zeros((half, own), jnp.float32)
        for n in range(slots):
            count = count + jnp.where(slots_ref[n : n + 1, :] == name, 1.0, 0.0)
        oper_ref[rows, :own] = count * moment_re
        oper_ref[rows, own:] = count * moment_im
        degree_ref[...] += jnp.sum(count * energy, axis=0, keepdims=True)
        scale = 1.0 / (energy + EPS)
        ar_ref[rows, :] = moment_re * scale
        ai_ref[rows, :] = moment_im * scale
        return 0

    lax.fori_loop(0, 2 * blocks, tile, 0)

    names = slots_t_ref[...]
    lane = names % wide
    owner = names // wide

    def pick(block, found):
        rows = pl.ds(pl.multiple_of(block * wide, wide), wide)
        here = owner == block
        got_re = jnp.take_along_axis(ar_ref[rows, :].T, lane, axis=1, mode="promise_in_bounds")
        got_im = jnp.take_along_axis(ai_ref[rows, :].T, lane, axis=1, mode="promise_in_bounds")
        return (jnp.where(here, got_re, found[0]), jnp.where(here, got_im, found[1]))

    zero = jnp.zeros(names.shape, jnp.float32)
    found = lax.fori_loop(0, blocks, pick, (zero, zero))
    align_ref[0] = found[0].T[:slots]
    align_ref[1] = found[1].T[:slots]


def whiten_kernel(gram_ref, image_ref, out_ref):
    order = gram_ref.shape[0]
    lanes = image_ref.shape[1]
    gram = gram_ref[...]
    right = jnp.concatenate([image_ref[:order], image_ref[order:]], axis=1)
    row = lax.broadcasted_iota(jnp.int32, (order, 1), 0)
    for p in range(order):
        pivot = gram[p : p + 1, p : p + 1]
        factor = jnp.where(row > p, gram[:, p : p + 1] / pivot, 0.0)
        scale = jnp.where(row == p, lax.rsqrt(pivot), 1.0)
        new_right = (right - factor * right[p : p + 1]) * scale
        gram = gram - factor * gram[p : p + 1]
        right = new_right
    out_ref[:order] = right[:, :lanes]
    out_ref[order:] = right[:, lanes:]


def shards(coefficients, truncation, neighbours, initial):
    highest = lax.Precision.HIGHEST
    groups = lax.axis_size("grp")
    replicas = lax.axis_size("rep")
    particles = coefficients.shape[0]
    slots = neighbours.shape[0]
    total = particles * groups * replicas
    in_group = neighbours - lax.axis_index("grp") * (replicas * particles)
    padded = jnp.pad(in_group.T, ((0, 0), (0, 128 - slots)))

    mine = coefficients.reshape(particles, 2 * RAD, ANG).transpose(2, 1, 0)
    everyone = lax.all_gather(mine, "rep", axis=0)
    kept = jnp.arange(ANG, dtype=jnp.int32)[:, None] < truncation[None, :]
    kept = jnp.concatenate([kept, kept], axis=1)[:, :, None]
    turned = jnp.concatenate([mine[:, RAD:], -mine[:, :RAD]], axis=1)
    own = jnp.concatenate([mine, turned], axis=2)
    own = jnp.where(kept, own, jnp.zeros_like(own))

    group = replicas * particles
    alignment, operator, degree = pl.pallas_call(
        moments_kernel,
        out_shape=[
            jax.ShapeDtypeStruct((2, slots, particles), jnp.float32),
            jax.ShapeDtypeStruct((group, 2 * particles), jnp.float32),
            jax.ShapeDtypeStruct((1, particles), jnp.float32),
        ],
        in_specs=[VMEM] * 4,
        out_specs=[VMEM] * 3,
        scratch_shapes=[pltpu.VMEM((group, particles), jnp.float32)] * 2,
        name="moments",
    )(own, everyone, in_group, padded)

    count = initial.shape[0] // 2
    current = initial
    for _ in range(ITERS):
        whole = lax.all_gather(current, "rep", axis=1, tiled=True)
        product = jnp.dot(whole, operator, precision=highest)
        image_re = product[:count, :particles] - product[count:, particles:]
        image_im = product[count:, :particles] + product[:count, particles:]
        current = jnp.concatenate([image_re, image_im], axis=0) / degree
    image_re, image_im = current[:count], current[count:]
    gram = lax.psum(
        (jnp.dot(image_re, image_re.T, precision=highest) + jnp.dot(image_im, image_im.T, precision=highest)) / total,
        ("grp", "rep"),
    )
    vectors = pl.pallas_call(
        whiten_kernel,
        out_shape=jax.ShapeDtypeStruct(initial.shape, jnp.float32),
        in_specs=[VMEM] * 2,
        out_specs=VMEM,
        name="whiten",
    )(gram, current)
    return alignment, vectors


def solution(mesh):
    in_specs = (P(("grp", "rep"), None), P(), P(None, ("grp", "rep")), P(None, ("grp", "rep")))
    out_specs = (P(None, None, ("grp", "rep")), P(None, ("grp", "rep")))
    return jax.shard_map(shards, mesh=mesh, in_specs=in_specs, out_specs=out_specs, check_vma=False)
```

time: 807 us -> 229 us (0.28)
  other arithmetic: 406 us -> 3.11 us
  local copies, waits for them, and re-layouts: 210 us -> 4.6 us
  Pallas kernels: 0 us -> 32.1 us
  waiting for transfers between devices: 22 us -> 39.7 us
    div x8 -> x3, other arithmetic: 255 us -> 0.68 us  [shards(): current = jnp.concatenate([image_re, image_im], axis=0) / degree]
    gather x11 -> x0, local copies, waits for them, and re-layouts: 183 us -> none  [the longest x8 145 us: one_block(): other_rows = jnp.take(rows_all, indices.reshape(-1), axis=0)]
    convert_element_type x13 -> x0, other arithmetic: 63.7 us -> none  [the longest x4 59.1 us: pair_moments(): partner = other_rows.reshape(NB, row_count, 2, RAD, ANG).astype(jnp.float32)]
    reduce_sum x8 -> x0, other arithmetic: 59.9 us -> none  [the longest x4 50.6 us: pair_moments(): jnp.sum(own_real * partner_real + own_imag * partner_imag, axis=2)]
    pallas_call x0 -> x2, Pallas kernels: none -> 32.1 us  [the longest x1 29.6 us: shards(): pl.pallas_call(moments_kernel, out_shape=[jax.ShapeDtypeStruct((2, slots,...]
    slice x27 -> x0, local copies, waits for them, and re-layouts: 22.9 us -> none  [the longest x15 10.6 us: lower_inverse(): running = running - lower[target, source] * inverse_rows[source]]
    all_gather x1, waiting for transfers between devices: 21.3 us -> 39.7 us  [shards(): everyone = lax.all_gather(mine, 'rep', axis=0)]
    select_n x11 -> x1, other arithmetic: 17.8 us -> 1.23 us  [shards(): own = jnp.where(kept, own, jnp.zeros_like(own))]
  transfers between devices with their start and end apart: 1 -> 1, of which waited for: 1 -> 1; matrix products, arithmetic and copies ran while one was open for 3% -> 2% of each run, Pallas kernels for 0% -> 0%
where the time goes in v1:
time: 229 us
  blocking collectives  131 us (57%)
  waiting for transfers between devices  39.7 us (17%)
  Pallas kernels  32.1 us (14%)
  between operations  14.2 us (6%)
  local copies, waits for them, and re-layouts  4.6 us (2%)
  matrix products  3.39 us (1%)
  other arithmetic  3.11 us (1%)
    all_gather x3, blocking collectives, shards(): whole = lax.all_gather(current, 'rep', axis=1, tiled=True)  94.1 us
    all_gather x1, waiting for transfers between devices, shards(): everyone = lax.all_gather(mine, 'rep', axis=0)  39.7 us
    psum x1, blocking collectives, shards(): lax.psum((jnp.dot(image_re, image_re.T, precision=highest) + jnp.dot(imag...  37.3 us
    pallas_call x1, Pallas kernels, shards(): pl.pallas_call(moments_kernel, out_shape=[jax.ShapeDtypeStruct((2, slots,...  29.6 us
  transfers between devices with their start and end apart: 1, of which 1 were waited for; matrix products, arithmetic and copies ran while one was open for 2% of the time, Pallas kernels for 0%

profile of v1, /device:TPU:0, one launch (start us, length us, event | category | flops | bytes accessed | tf_op | source)
XLA Modules:
  0.0 228.6 jit_solution(12435329072555756733)
XLA Ops:
  7.2 0.0 copy-start.4
  7.2 0.0 copy-start.5
  7.2 0.0 copy-start.7
  7.2 0.0 all-gather.3.cloned.1.call-start
  7.2 1.3 copy.19
  8.6 1.2 copy.26
  9.7 0.0 all-gather.3.cloned.1.call-update
  9.8 0.0 copy-done.4
  9.8 0.1 copy.21
  9.9 0.7 copy.23.slots_ref
  10.6 0.6 pad.4.slots_t_ref
  11.2 0.0 copy-done.5
  11.2 33.1 %all_gather.17 = f32[32,1024]{1,0:T(8,128)S(1)} all-gather(f32[32,128]{1,0:T(8,128)S(1)} %copy-done.5), channel_id=1, replica_groups=mesh['grp'=4,'rep'=8] {'rep'}, dimensions={1}, use_global_device_ids=true | all-gather | bytes 147456 | tf_op jit(solution)/shard_map/all_gather | solution.py:133
  44.3 0.0 copy-done.7
  44.3 0.1 pad_add_fusion
  44.4 1.1 fusion.4
  45.5 0.0 copy-done.1
  45.5 1.2 maximum_select_fusion.own_ref
  46.7 39.7 %all-gather.3.cloned.1.call-done = bf16[512,32,128]{2,1,0:T(8,128)(2,1)} async-done(((bf16[64,32,128]{2,1,0:T(8,128)(2,1)}), bf16[512,32,128]{2,1,0:T(8,128)(2,1)}) %all-gather.3.cloned.1.call-update) | async-done | bytes 4194320 | tf_op jit(solution)/shard_map/all_gather | solution.py:109
  86.5 29.6 %moments.1 = (f32[2,50,128]{2,1,0:T(8,128)}, f32[1024,256]{1,0:T(8,128)}, f32[1,128]{1,0:T(1,128)}) custom-call(bf16[64,32,256]{2,1,0:T(8,128)(2,1)} %maximum_select_fusion.own_ref, bf16[8,64,32,128]{3,2,1,0:T(8,128)(2,1)} %bitcast.19, s32[50,128]{1,0:T(8,128)} %copy.23.slots_ref, s32[128,128]{1,0:T(8,128)} %pad.4.slots_t_ref), custom_call_target="tpu_custom_call" | custom-call | tf_op jit(solution)/shard_map/moments/pallas_call | solution.py:117
  116.0 2.0 convolution_bitcast_fusion
  118.0 0.7 maximum_divide_fusion
  118.7 30.5 %all_gather.18 = f32[32,1024]{1,0:T(8,128)S(1)} all-gather(f32[32,128]{1,0:T(8,128)S(1)} %maximum_divide_fusion), channel_id=1, replica_groups=mesh['grp'=4,'rep'=8] {'rep'}, dimensions={1}, use_global_device_ids=true | all-gather | bytes 147456 | tf_op jit(solution)/shard_map/all_gather | solution.py:133
  149.2 0.6 fusion.5
  149.8 30.5 %all_gather.19 = f32[32,1024]{1,0:T(8,128)S(1)} all-gather(f32[32,128]{1,0:T(8,128)S(1)} %maximum_divide_fusion.1), channel_id=1, replica_groups=mesh['grp'=4,'rep'=8] {'rep'}, dimensions={1}, use_global_device_ids=true | all-gather | bytes 147456 | tf_op jit(solution)/shard_map/all_gather | solution.py:133
  180.3 0.6 fusion.6
  181.0 0.0 copy-start.2
  181.0 0.1 fusion.2
  181.1 0.1 fusion
  181.2 37.3 %psum.7.gram_ref = f32[16,16]{1,0:T(8,128)} all-reduce(f32[16,16]{1,0:T(8,128)S(1)} %fusion), channel_id=1, replica_groups=mesh['grp'=4,'rep'=8] {'grp','rep'}, use_global_device_ids=true, to_apply=%region_0.1 | all-reduce | flops 256 | bytes 2048 | tf_op jit(solution)/shard_map/psum | solution.py:139
  218.5 2.6 %whiten.1 = f32[32,128]{1,0:T(8,128)} custom-call(f32[16,16]{1,0:T(8,128)} %psum.7.gram_ref, f32[32,128]{1,0:T(8,128)} %copy-done.2), custom_call_target="tpu_custom_call" | custom-call | tf_op jit(solution)/shard_map/whiten/pallas_call | solution.py:143
  221.1 0.6 copy.24
  (16 shorter events, 0.1 us)
Async XLA Ops:
  7.2 2.6 %copy-start.4 = (s32[50,128]{1,0:T(8,128)S(1)}, s32[50,128]{1,0:T(8,128)}, u32[]{:S(2)}) copy-start(s32[50,128]{1,0:T(8,128)} %param.6) | copy-start | bytes 76804
  7.2 4.1 %copy-start.5 = (f32[32,128]{1,0:T(8,128)S(1)}, f32[32,128]{1,0:T(8,128)}, u32[]{:S(2)}) copy-start(f32[32,128]{1,0:T(8,128)} %param.7) | copy-start | bytes 49156
  7.2 37.1 %copy-start.7 = (s32[16]{0:T(128)S(1)}, s32[16]{0:T(128)}, u32[]{:S(2)}) copy-start(s32[16]{0:T(128)} %param.5) | copy-start | bytes 196
  7.2 79.3 %all-gather.3.cloned.1.call-start = ((), (), s32[]{:S(2)}) async-start(), calls=%async_computation | async-start | bytes 4718592 | tf_op jit(solution)/shard_map/all_gather | solution.py:109
  9.7 35.7 %copy-start.1 = (bf16[128,32,64]{0,1,2:T(8,128)(2,1)S(1)}, bf16[128,32,64]{0,1,2:T(8,128)(2,1)}, u32[]{:S(2)}) copy-start(bf16[128,32,64]{0,1,2:T(8,128)(2,1)} %copy.26) | copy-start | bytes 1572868
  116.0 33.2 %copy-start = (f32[1024,256]{1,0:T(8,128)S(1)}, f32[1024,256]{1,0:T(8,128)}, u32[]{:S(2)}) copy-start(f32[1024,256]{1,0:T(8,128)} %get-tuple-element.6) | copy-start | bytes 3145732
  116.0 33.8 %copy-start.6 = (f32[1,128]{1,0:T(1,128)S(1)}, f32[1,128]{1,0:T(1,128)}, u32[]{:S(2)}) copy-start(f32[1,128]{1,0:T(1,128)} %get-tuple-element.7) | copy-start | bytes 1540
  116.0 105.1 %copy-start.3 = (f32[2,50,128]{2,1,0:T(8,128)S(1)}, f32[2,50,128]{2,1,0:T(8,128)}, u32[]{:S(2)}) copy-start(f32[2,50,128]{2,1,0:T(8,128)} %get-tuple-element.14) | copy-start | bytes 153604
  181.0 37.6 %copy-start.2 = (f32[32,128]{1,0:T(8,128)}, f32[32,128]{1,0:T(8,128)S(1)}, u32[]{:S(2)}) copy-start(f32[32,128]{1,0:T(8,128)S(1)} %maximum_divide_fusion.2.image_ref) | copy-start | bytes 49156
Sparse Core Ops, SparseCore 0:
  10.1 76.2 all-gather.2

commit v2 on v1

--- a/solution.py
+++ b/solution.py
@@ -12,6 +12,7 @@
 RAD = 16
 ITERS = 3
 EPS = 1e-06
+MESH = pl.DeviceIdType.MESH
 VMEM = pl.BlockSpec(memory_space=pltpu.VMEM)
 
 
@@ -78,30 +79,101 @@
     align_ref[1] = found[1].T[:slots]
 
 
-def whiten_kernel(gram_ref, image_ref, out_ref):
-    order = gram_ref.shape[0]
-    lanes = image_ref.shape[1]
-    gram = gram_ref[...]
-    right = jnp.concatenate([image_ref[:order], image_ref[order:]], axis=1)
+def diffuse_kernel(oper_ref, degree_ref, initial_ref, out_ref, land, image, part_gram, land_rep, land_grp, *sems):
+    send, recv, send_rep, recv_rep, send_grp, recv_grp = sems
+    groups, replicas = lax.axis_size("grp"), lax.axis_size("rep")
+    grp, rep = lax.axis_index("grp"), lax.axis_index("rep")
+    rows, particles = initial_ref.shape
+    order = rows // 2
+    highest = lax.Precision.HIGHEST
+
+    def on_rep(step):
+        return (grp, lax.rem(rep + step, replicas))
+
+    def on_grp(step):
+        return (lax.rem(grp + step, groups), rep)
+
+    barrier = pltpu.get_barrier_semaphore()
+    for step in range(1, replicas):
+        pl.semaphore_signal(barrier, inc=1, device_id=on_rep(step), device_id_type=MESH)
+    for step in range(1, groups):
+        pl.semaphore_signal(barrier, inc=1, device_id=on_grp(step), device_id_type=MESH)
+    pl.semaphore_wait(barrier, replicas + groups - 2)
+
+    def spread(src, dst, out_sems, in_sems, peer, count):
+        copies = []
+        for step in range(1, count):
+            copy = pltpu.make_async_remote_copy(
+                src_ref=src,
+                dst_ref=dst,
+                send_sem=out_sems.at[step],
+                recv_sem=in_sems.at[step],
+                device_id=peer(step),
+                device_id_type=MESH,
+            )
+            copy.start()
+            copies.append(copy)
+        return copies
+
+    started = []
+    for turn in range(ITERS):
+        src = initial_ref if turn == 0 else image.at[turn - 1]
+        copies = spread(src, land.at[turn, rep], send.at[turn], recv.at[turn], on_rep, replicas)
+        land[turn, pl.ds(rep, 1)] = src[...][None]
+        started += copies
+        for copy in copies:
+            copy.wait_recv()
+        whole = jnp.concatenate([land[turn, r] for r in range(replicas)], axis=1)
+        product = jnp.dot(whole, oper_ref[...], precision=highest, preferred_element_type=jnp.float32)
+        image_re = (product[:order, :particles] - product[order:, particles:]) / degree_ref[...]
+        image_im = (product[order:, :particles] + product[:order, particles:]) / degree_ref[...]
+        if turn < ITERS - 1:
+            image[turn, :order] = image_re
+            image[turn, order:] = image_im
+
+    right = jnp.concatenate([image_re, image_im], axis=1)
+    tall = jnp.concatenate([right, jnp.zeros((128 - order, right.shape[1]), jnp.float32)], axis=0)
+    gram = lax.dot_general(
+        right, tall, (((1,), (1,)), ((), ())), precision=highest, preferred_element_type=jnp.float32
+    )
+    part_gram[0] = gram
+    land_rep[pl.ds(rep, 1)] = gram[None]
+    copies = spread(part_gram.at[0], land_rep.at[rep], send_rep, recv_rep, on_rep, replicas)
+    started += copies
+    for copy in copies:
+        copy.wait_recv()
+    gram = land_rep[0]
+    for r in range(1, replicas):
+        gram = gram + land_rep[r]
+    part_gram[1] = gram
+    land_grp[pl.ds(grp, 1)] = gram[None]
+    copies = spread(part_gram.at[1], land_grp.at[grp], send_grp, recv_grp, on_grp, groups)
+    started += copies
+    for copy in copies:
+        copy.wait_recv()
+    gram = land_grp[0]
+    for g in range(1, groups):
+        gram = gram + land_grp[g]
+    gram = gram * (1.0 / (particles * groups * replicas))
+
     row = lax.broadcasted_iota(jnp.int32, (order, 1), 0)
     for p in range(order):
         pivot = gram[p : p + 1, p : p + 1]
         factor = jnp.where(row > p, gram[:, p : p + 1] / pivot, 0.0)
         scale = jnp.where(row == p, lax.rsqrt(pivot), 1.0)
-        new_right = (right - factor * right[p : p + 1]) * scale
+        right = (right - factor * right[p : p + 1]) * scale
         gram = gram - factor * gram[p : p + 1]
-        right = new_right
-    out_ref[:order] = right[:, :lanes]
-    out_ref[order:] = right[:, lanes:]
+    out_ref[:order] = right[:, :particles]
+    out_ref[order:] = right[:, particles:]
+    for copy in started:
+        copy.wait_send()
 
 
 def shards(coefficients, truncation, neighbours, initial):
-    highest = lax.Precision.HIGHEST
     groups = lax.axis_size("grp")
     replicas = lax.axis_size("rep")
     particles = coefficients.shape[0]
     slots = neighbours.shape[0]
-    total = particles * groups * replicas
     in_group = neighbours - lax.axis_index("grp") * (replicas * particles)
     padded = jnp.pad(in_group.T, ((0, 0), (0, 128 - slots)))
 
@@ -127,26 +199,29 @@
         name="moments",
     )(own, everyone, in_group, padded)
 
-    count = initial.shape[0] // 2
-    current = initial
-    for _ in range(ITERS):
-        whole = lax.all_gather(current, "rep", axis=1, tiled=True)
-        product = jnp.dot(whole, operator, precision=highest)
-        image_re = product[:count, :particles] - product[count:, particles:]
-        image_im = product[count:, :particles] + product[:count, particles:]
-        current = jnp.concatenate([image_re, image_im], axis=0) / degree
-    image_re, image_im = current[:count], current[count:]
-    gram = lax.psum(
-        (jnp.dot(image_re, image_re.T, precision=highest) + jnp.dot(image_im, image_im.T, precision=highest)) / total,
-        ("grp", "rep"),
-    )
+    rows = initial.shape[0]
+    order = rows // 2
     vectors = pl.pallas_call(
-        whiten_kernel,
+        diffuse_kernel,
         out_shape=jax.ShapeDtypeStruct(initial.shape, jnp.float32),
-        in_specs=[VMEM] * 2,
+        in_specs=[VMEM] * 3,
         out_specs=VMEM,
-        name="whiten",
-    )(gram, current)
+        scratch_shapes=[
+            pltpu.VMEM((ITERS, replicas, rows, particles), jnp.float32),
+            pltpu.VMEM((ITERS - 1, rows, particles), jnp.float32),
+            pltpu.VMEM((2, order, 128), jnp.float32),
+            pltpu.VMEM((replicas, order, 128), jnp.float32),
+            pltpu.VMEM((groups, order, 128), jnp.float32),
+            pltpu.SemaphoreType.DMA((ITERS, replicas)),
+            pltpu.SemaphoreType.DMA((ITERS, replicas)),
+            pltpu.SemaphoreType.DMA((replicas,)),
+            pltpu.SemaphoreType.DMA((replicas,)),
+            pltpu.SemaphoreType.DMA((groups,)),
+            pltpu.SemaphoreType.DMA((groups,)),
+        ],
+        compiler_params=pltpu.CompilerParams(collective_id=0, has_side_effects=True),
+        name="diffuse",
+    )(operator, degree, initial)
     return alignment, vectors
 
 

time: 229 us -> 155 us (0.68)
  blocking collectives: 131 us -> 0 us
  waiting for transfers between devices: 39.7 us -> 72.1 us
  Pallas kernels: 32.1 us -> 59.2 us
  matrix products: 3.39 us -> 0 us
    all_gather x3 -> x0, blocking collectives: 94.1 us -> none  [shards(): whole = lax.all_gather(current, 'rep', axis=1, tiled=True)]
    psum x1 -> x0, blocking collectives: 37.3 us -> none  [shards(): lax.psum((jnp.dot(image_re, image_re.T, precision=highest) + jnp.dot(imag...]
    all_gather x1, waiting for transfers between devices: 39.7 us -> 72 us  [shards(): everyone = lax.all_gather(mine, 'rep', axis=0)]
    pallas_call x1, Pallas kernels: 2.58 us -> 29.6 us  [shards(): pl.pallas_call(diffuse_kernel, out_shape=jax.ShapeDtypeStruct(initial.sha...]
    dot_general x5 -> x0, matrix products: 3.39 us -> none  [the longest x3 3.13 us: shards(): product = jnp.dot(whole, operator, precision=highest)]
where the time goes in v2:
time: 155 us; the launch traced here: 154 us
  waiting for transfers between devices  72.1 us (47%)
  Pallas kernels  59.2 us (38%)
  between operations  14.1 us (9%)
  local copies, waits for them, and re-layouts  6.69 us (4%)
  other arithmetic  2.42 us (2%)
    all_gather x1, waiting for transfers between devices, shards(): everyone = lax.all_gather(mine, 'rep', axis=0)  72 us
    pallas_call x1, Pallas kernels, shards(): pl.pallas_call(diffuse_kernel, out_shape=jax.ShapeDtypeStruct(initial.sha...  29.6 us
    pallas_call x1, Pallas kernels, shards(): pl.pallas_call(moments_kernel, out_shape=[jax.ShapeDtypeStruct((2, slots,...  29.6 us
    unnamed x10, local copies, waits for them, and re-layouts  4.21 us
  transfers between devices with their start and end apart: 1, of which 1 were waited for; matrix products, arithmetic and copies ran while one was open for 2% of the time, Pallas kernels for 0%

profile of v2, /device:TPU:0, one launch (start us, length us, event | category | flops | bytes accessed | tf_op | source)
XLA Modules:
  0.0 154.5 jit_solution(394446652815688406)
XLA Ops:
  7.2 0.0 copy-start.1
  7.2 0.0 copy-start.2
  7.2 0.0 all-gather.3.cloned.1.call-start
  7.2 1.3 copy.19
  8.5 1.2 copy.26
  9.7 0.0 copy-start
  9.7 0.0 all-gather.3.cloned.1.call-update
  9.7 0.0 copy-done.1
  9.7 0.1 copy.21
  9.9 0.7 copy.23.slots_ref
  10.6 0.6 pad.4.slots_t_ref
  11.2 0.0 copy-done.2
  11.2 0.1 pad_add_fusion
  11.3 1.1 fusion
  12.4 0.0 copy-done
  12.4 1.2 maximum_select_fusion.own_ref
  13.6 72.0 %all-gather.3.cloned.1.call-done = bf16[512,32,128]{2,1,0:T(8,128)(2,1)} async-done(((bf16[64,32,128]{2,1,0:T(8,128)(2,1)}), bf16[512,32,128]{2,1,0:T(8,128)(2,1)}) %all-gather.3.cloned.1.call-update) | async-done | bytes 4194320 | tf_op jit(solution)/shard_map/all_gather | solution.py:181
  85.7 29.6 %moments.1 = (f32[2,50,128]{2,1,0:T(8,128)}, f32[1024,256]{1,0:T(8,128)}, f32[1,128]{1,0:T(1,128)}) custom-call(bf16[64,32,256]{2,1,0:T(8,128)(2,1)} %maximum_select_fusion.own_ref, bf16[8,64,32,128]{3,2,1,0:T(8,128)(2,1)} %bitcast.10, s32[50,128]{1,0:T(8,128)} %copy.23.slots_ref, s32[128,128]{1,0:T(8,128)} %pad.4.slots_t_ref), custom_call_target="tpu_custom_call" | custom-call | tf_op jit(solution)/shard_map/moments/pallas_call | solution.py:189
  115.2 1.5 copy.24
  116.7 29.6 %diffuse.1 = f32[32,128]{1,0:T(8,128)} custom-call(f32[1024,256]{1,0:T(8,128)} %get-tuple-element.6.oper_ref, f32[1,128]{1,0:T(1,128)} %get-tuple-element.7.degree_ref, f32[32,128]{1,0:T(8,128)} %initial_ref.1), custom_call_target="tpu_custom_call" | custom-call | tf_op jit(solution)/shard_map/diffuse/pallas_call | solution.py:204
  146.3 1.3 copy.28
  (3 shorter events, 0.0 us)
Async XLA Ops:
  7.2 2.6 %copy-start.1 = (s32[50,128]{1,0:T(8,128)S(1)}, s32[50,128]{1,0:T(8,128)}, u32[]{:S(2)}) copy-start(s32[50,128]{1,0:T(8,128)} %param.6) | copy-start | bytes 76804
  7.2 4.0 %copy-start.2 = (s32[16]{0:T(128)S(1)}, s32[16]{0:T(128)}, u32[]{:S(2)}) copy-start(s32[16]{0:T(128)} %param.5) | copy-start | bytes 196
  7.2 78.5 %all-gather.3.cloned.1.call-start = ((), (), s32[]{:S(2)}) async-start(), calls=%async_computation | async-start | bytes 4718592 | tf_op jit(solution)/shard_map/all_gather | solution.py:181
  9.7 2.7 %copy-start = (bf16[128,32,64]{0,1,2:T(8,128)(2,1)S(1)}, bf16[128,32,64]{0,1,2:T(8,128)(2,1)}, u32[]{:S(2)}) copy-start(bf16[128,32,64]{0,1,2:T(8,128)(2,1)} %copy.26) | copy-start | bytes 1572868
Sparse Core Ops, SparseCore 0:
  10.1 75.4 all-gather.2

commit v3 on v2

v3 whole, which is shorter than its diff:
```python
import functools
import math

import jax
import jax.numpy as jnp
from jax import lax
from jax.experimental import pallas as pl
from jax.experimental.pallas import tpu as pltpu
from jax.sharding import PartitionSpec as P

ANG = 64
RAD = 16
ITERS = 3
EPS = 1e-06
MESH = pl.DeviceIdType.MESH
VMEM = pl.BlockSpec(memory_space=pltpu.VMEM)


def ring_name(place, across, along):
    column = place // along
    step = place % along
    return (step + (column % 2) * (along - 1 - 2 * step)) * across + column


def ring_place(name, across, along):
    row = name // across
    column = name % across
    return column * along + row + (column % 2) * (along - 1 - 2 * row)


def main_kernel(
    own_ref, mine_ref, slots_ref, initial_ref, ar_ref, ai_ref, out_ref,
    blocks, oper_ref, degree_ref, land, image, part_gram, land_rep, land_grp,
    copy_sem, ring_send, ring_recv, send, recv, send_rep, recv_rep, send_grp, recv_grp,
):
    groups, replicas = lax.axis_size("grp"), lax.axis_size("rep")
    grp, rep = lax.axis_index("grp"), lax.axis_index("rep")
    rows, particles = initial_ref.shape
    order = rows // 2
    highest = lax.Precision.HIGHEST
    own = own_ref.shape[2] // 2
    slots = slots_ref.shape[0]
    half = particles // 2
    along = math.gcd(replicas, 4)
    across = replicas // along
    middle = replicas // 2
    chunk = ANG // 2
    place = ring_place(rep, across, along)
    right_rep = ring_name((place + 1) % replicas, across, along)
    left_rep = ring_name((place + replicas - 1) % replicas, across, along)

    to_first = pltpu.make_async_copy(mine_ref, blocks.at[0], copy_sem)
    to_first.start()

    def on_rep(step):
        return (grp, lax.rem(rep + step, replicas))

    def on_grp(step):
        return (lax.rem(grp + step, groups), rep)

    barrier = pltpu.get_barrier_semaphore()
    for step in range(1, replicas):
        pl.semaphore_signal(barrier, inc=1, device_id=on_rep(step), device_id_type=MESH)
    for step in range(1, groups):
        pl.semaphore_signal(barrier, inc=1, device_id=on_grp(step), device_id_type=MESH)
    pl.semaphore_wait(barrier, replicas + groups - 2)

    def hop(source, slot, part, peer):
        here = pl.ds(part * chunk, chunk)
        return pltpu.make_async_remote_copy(
            src_ref=source.at[here],
            dst_ref=blocks.at[slot, here],
            send_sem=ring_send.at[slot, part],
            recv_sem=ring_recv.at[slot, part],
            device_id=(grp, peer),
            device_id_type=MESH,
        )

    def spread(src, dst, out_sems, in_sems, peer, count):
        copies = []
        for step in range(1, count):
            copy = pltpu.make_async_remote_copy(
                src_ref=src,
                dst_ref=dst,
                send_sem=out_sems.at[step],
                recv_sem=in_sems.at[step],
                device_id=peer(step),
                device_id_type=MESH,
            )
            copy.start()
            copies.append(copy)
        return copies

    first_copies = spread(initial_ref, land.at[0, rep], send.at[0], recv.at[0], on_rep, replicas)
    for part in range(2):
        hop(mine_ref, 1, part, right_rep).start()
        hop(mine_ref, replicas - 1, part, left_rep).start()

    to_first.wait()
    degree_ref[...] = jnp.full(degree_ref.shape, EPS, jnp.float32)

    def block_step(turn, _):
        distance = (turn + 1) // 2
        odd = turn % 2

        @pl.when(jnp.logical_and(odd == 1, distance < middle))
        def _():
            back = replicas - distance
            for part in range(2):
                hop(mine_ref, distance, part, right_rep).wait_recv()

                @pl.when(distance + part < middle)
                def _():
                    hop(blocks.at[distance], distance + 1, part, right_rep).start()

                hop(mine_ref, back, part, left_rep).wait_recv()

                @pl.when(distance + 1 - part < middle)
                def _():
                    hop(blocks.at[back], back - 1, part, left_rep).start()

        @pl.when(jnp.logical_and(odd == 1, distance == middle))
        def _():
            for part in range(2):
                hop(mine_ref, middle, part, right_rep).wait_recv()

        slot = (odd * distance + (1 - odd) * (replicas - distance)) % replicas
        owner = ring_name((place + replicas - slot) % replicas, across, along)

        def tile(part, _):
            energy = moment_re = moment_im = before_re = before_im = None
            for k in range(ANG):
                partner = blocks[slot, k].T
                partner = jnp.where(part == 0, partner[:half], partner[half:])
                spectrum = jnp.dot(partner, own_ref[k], preferred_element_type=jnp.float32)
                re, im = spectrum[:, :own], spectrum[:, own:]
                if k == 0:
                    energy = 2.0 * (re * re)
                    before_re = 2.0 * re
                    continue
                energy = energy + (re * re + im * im)
                if k == 1:
                    moment_re = before_re * re
                    moment_im = -(before_re * im)
                else:
                    moment_re = moment_re + (before_re * re + before_im * im)
                    moment_im = moment_im + (before_im * re - before_re * im)
                before_re, before_im = re, im
            energy, moment_re, moment_im = 0.5 * energy, 0.5 * moment_re, 0.5 * moment_im
            first = pl.multiple_of(owner * particles + part * half, half)
            here = pl.ds(first, half)
            name = lax.broadcasted_iota(jnp.int32, (half, own), 0) + first
            count = jnp.zeros((half, own), jnp.float32)
            for n in range(slots):
                count = count + jnp.where(slots_ref[n : n + 1, :] == name, 1.0, 0.0)
            oper_ref[here, :own] = count * moment_re
            oper_ref[here, own:] = count * moment_im
            degree_ref[...] += jnp.sum(count * energy, axis=0, keepdims=True)
            scale = 1.0 / (energy + EPS)
            ar_ref[here, :] = moment_re * scale
            ai_ref[here, :] = moment_im * scale
            return 0

        lax.fori_loop(0, 2, tile, 0)
        return 0

    lax.fori_loop(0, replicas, block_step, 0)

    started = []
    for turn in range(ITERS):
        src = initial_ref if turn == 0 else image.at[turn - 1]
        if turn == 0:
            copies = first_copies
        else:
            copies = spread(src, land.at[turn, rep], send.at[turn], recv.at[turn], on_rep, replicas)
        land[turn, pl.ds(rep, 1)] = src[...][None]
        started += copies
        for copy in copies:
            copy.wait_recv()
        whole = jnp.concatenate([land[turn, r] for r in range(replicas)], axis=1)
        product = jnp.dot(whole, oper_ref[...], precision=highest, preferred_element_type=jnp.float32)
        image_re = (product[:order, :particles] - product[order:, particles:]) / degree_ref[...]
        image_im = (product[order:, :particles] + product[:order, particles:]) / degree_ref[...]
        if turn < ITERS - 1:
            image[turn, :order] = image_re
            image[turn, order:] = image_im

    right = jnp.concatenate([image_re, image_im], axis=1)
    tall = jnp.concatenate([right, jnp.zeros((128 - order, right.shape[1]), jnp.float32)], axis=0)
    gram = lax.dot_general(
        right, tall, (((1,), (1,)), ((), ())), precision=highest, preferred_element_type=jnp.float32
    )
    part_gram[0] = gram
    land_rep[pl.ds(rep, 1)] = gram[None]
    copies = spread(part_gram.at[0], land_rep.at[rep], send_rep, recv_rep, on_rep, replicas)
    started += copies
    for copy in copies:
        copy.wait_recv()
    gram = land_rep[0]
    for r in range(1, replicas):
        gram = gram + land_rep[r]
    part_gram[1] = gram
    land_grp[pl.ds(grp, 1)] = gram[None]
    copies = spread(part_gram.at[1], land_grp.at[grp], send_grp, recv_grp, on_grp, groups)
    started += copies
    for copy in copies:
        copy.wait_recv()
    gram = land_grp[0]
    for g in range(1, groups):
        gram = gram + land_grp[g]
    gram = gram * (1.0 / (particles * groups * replicas))

    row = lax.broadcasted_iota(jnp.int32, (order, 1), 0)
    for p in range(order):
        pivot = gram[p : p + 1, p : p + 1]
        factor = jnp.where(row > p, gram[:, p : p + 1] / pivot, 0.0)
        scale = jnp.where(row == p, lax.rsqrt(pivot), 1.0)
        right = (right - factor * right[p : p + 1]) * scale
        gram = gram - factor * gram[p : p + 1]
    out_ref[:order] = right[:, :particles]
    out_ref[order:] = right[:, particles:]
    for copy in started:
        copy.wait_send()
    for part in range(2):
        for distance in range(1, replicas):
            if distance != middle:
                hop(mine_ref, distance, part, right_rep).wait_send()
        hop(mine_ref, middle, part, right_rep).wait_send()


def pick_kernel(ar_ref, ai_ref, slots_t_ref, align_ref):
    slots, wide = align_ref.shape[1:]
    names = slots_t_ref[...]
    lane = names % wide
    owner = names // wide

    def pick(block, found):
        rows = pl.ds(pl.multiple_of(block * wide, wide), wide)
        here = owner == block
        got_re = jnp.take_along_axis(ar_ref[rows, :].T, lane, axis=1, mode="promise_in_bounds")
        got_im = jnp.take_along_axis(ai_ref[rows, :].T, lane, axis=1, mode="promise_in_bounds")
        return (jnp.where(here, got_re, found[0]), jnp.where(here, got_im, found[1]))

    zero = jnp.zeros(names.shape, jnp.float32)
    found = lax.fori_loop(0, ar_ref.shape[0] // wide, pick, (zero, zero))
    align_ref[0] = found[0].T[:slots]
    align_ref[1] = found[1].T[:slots]


def shards(coefficients, truncation, neighbours, initial):
    groups = lax.axis_size("grp")
    replicas = lax.axis_size("rep")
    particles = coefficients.shape[0]
    slots = neighbours.shape[0]
    in_group = neighbours - lax.axis_index("grp") * (replicas * particles)
    padded = jnp.pad(in_group.T, ((0, 0), (0, 128 - slots)))

    mine = coefficients.reshape(particles, 2 * RAD, ANG).transpose(2, 1, 0)
    kept = jnp.arange(ANG, dtype=jnp.int32)[:, None] < truncation[None, :]
    kept = jnp.concatenate([kept, kept], axis=1)[:, :, None]
    turned = jnp.concatenate([mine[:, RAD:], -mine[:, :RAD]], axis=1)
    own = jnp.concatenate([mine, turned], axis=2)
    own = jnp.where(kept, own, jnp.zeros_like(own))

    group = replicas * particles
    rows = initial.shape[0]
    order = rows // 2
    dma = pltpu.SemaphoreType.DMA
    table = jax.ShapeDtypeStruct((group, particles), jnp.float32)
    ratio_re, ratio_im, vectors = pl.pallas_call(
        main_kernel,
        out_shape=[table, table, jax.ShapeDtypeStruct(initial.shape, jnp.float32)],
        in_specs=[VMEM] * 4,
        out_specs=[VMEM] * 3,
        scratch_shapes=[
            pltpu.VMEM((replicas,) + mine.shape, mine.dtype),
            pltpu.VMEM((group, 2 * particles), jnp.float32),
            pltpu.VMEM((1, particles), jnp.float32),
            pltpu.VMEM((ITERS, replicas, rows, particles), jnp.float32),
            pltpu.VMEM((ITERS - 1, rows, particles), jnp.float32),
            pltpu.VMEM((2, order, 128), jnp.float32),
            pltpu.VMEM((replicas, order, 128), jnp.float32),
            pltpu.VMEM((groups, order, 128), jnp.float32),
            dma,
            dma((replicas, 2)),
            dma((replicas, 2)),
            dma((ITERS, replicas)),
            dma((ITERS, replicas)),
            dma((replicas,)),
            dma((replicas,)),
            dma((groups,)),
            dma((groups,)),
        ],
        compiler_params=pltpu.CompilerParams(collective_id=0, has_side_effects=True),
        name="main",
    )(own, mine, in_group, initial)
    alignment = pl.pallas_call(
        pick_kernel,
        out_shape=jax.ShapeDtypeStruct((2, slots, particles), jnp.float32),
        in_specs=[VMEM] * 3,
        out_specs=VMEM,
        name="pick",
    )(ratio_re, ratio_im, padded)
    return alignment, vectors


def solution(mesh):
    in_specs = (P(("grp", "rep"), None), P(), P(None, ("grp", "rep")), P(None, ("grp", "rep")))
    out_specs = (P(None, None, ("grp", "rep")), P(None, ("grp", "rep")))
    return jax.shard_map(shards, mesh=mesh, in_specs=in_specs, out_specs=out_specs, check_vma=False)
```

time: 155 us -> 89.7 us (0.58)
  waiting for transfers between devices: 72.1 us -> 0 us
  Pallas kernels: 59.2 us -> 80.7 us
  between operations: 14.1 us -> 0.7 us
    all_gather x1 -> x0, waiting for transfers between devices: 72 us -> none  [shards(): everyone = lax.all_gather(mine, 'rep', axis=0)]
    pallas_call x2, Pallas kernels: 59.2 us -> 80.7 us  [the longest x1 77.1 us: shards(): pl.pallas_call(main_kernel, out_shape=[table, table, jax.ShapeDtypeStruct...]
    unnamed x10 -> x8, local copies, waits for them, and re-layouts: 4.21 us -> 4.23 us
  transfers between devices with their start and end apart: 1 -> 0, of which waited for: 1 -> 0; matrix products, arithmetic and copies ran while one was open for 2% -> 0% of each run, Pallas kernels for 0% -> 0%
where the time goes in v3:
time: 89.7 us; the launch traced here: 89.3 us
  Pallas kernels  80.7 us (90%)
  local copies, waits for them, and re-layouts  5.9 us (7%)
  other arithmetic  2.04 us (2%)
    pallas_call x1, Pallas kernels, shards(): pl.pallas_call(main_kernel, out_shape=[table, table, jax.ShapeDtypeStruct...  77.1 us
    unnamed x8, local copies, waits for them, and re-layouts  4.23 us
    pallas_call x1, Pallas kernels, shards(): pl.pallas_call(pick_kernel, out_shape=jax.ShapeDtypeStruct((2, slots, par...  3.62 us

profile of v3, /device:TPU:0, one launch (start us, length us, event | category | flops | bytes accessed | tf_op | source)
XLA Modules:
  0.0 89.3 jit_solution(17200655354100529284)
XLA Ops:
  0.6 0.7 iota_compare_fusion
  1.3 0.1 pad_add_fusion
  1.4 0.8 copy.16
  2.3 0.7 copy.18.slots_ref
  3.0 0.6 pad.4.slots_t_ref
  3.6 1.3 %copy.14 = bf16[128,2048]{0,1:T(8,128)(2,1)S(1)} copy(bf16[128,2048]{1,0:T(8,128)(2,1)} %param.4) | data formatting | bytes 1048576 | tf_op args[0]
  4.9 0.3 copy.21
  5.2 0.0 copy-start
  5.3 0.1 fusion
  5.3 1.2 %maximum_select_fusion.own_ref = bf16[64,32,256]{2,1,0:T(8,128)(2,1)} fusion(bf16[64,16,128]{2,1,0:T(8,128)(2,1)S(1)} %get-tuple-element.15, bf16[64,16,128]{2,1,0:T(8,128)(2,1)S(1)} %get-tuple-element.14, bf16[64,32,128]{2,1,0:T(8,128)(2,1)S(1)} %bitcast.7, pred[64,32]{1,0:T(8,128)(4,1)S(1)} %pad_add_fusion), kind=kLoop, calls=%fused_computation | loop fusion | flops 3670016 | bytes 2099200 | tf_op jit(solution)/shard_map/jit(_where)/select_n | solution.py:263
  6.5 0.0 copy-done
  6.5 77.1 %main.1 = (f32[1024,128]{1,0:T(8,128)}, f32[1024,128]{1,0:T(8,128)}, f32[32,128]{1,0:T(8,128)}) custom-call(bf16[64,32,256]{2,1,0:T(8,128)(2,1)} %maximum_select_fusion.own_ref, bf16[64,32,128]{2,1,0:T(8,128)(2,1)} %bitcast.8, s32[50,128]{1,0:T(8,128)} %copy.18.slots_ref, f32[32,128]{1,0:T(8,128)} %initial_ref.1), custom_call_target="tpu_custom_call" | custom-call | tf_op jit(solution)/shard_map/main/pallas_call | solution.py:270
  83.6 0.0 copy-start.1
  83.7 3.6 %pick.1 = f32[2,50,128]{2,1,0:T(8,128)} custom-call(f32[1024,128]{1,0:T(8,128)} %get-tuple-element.5.ar_ref, f32[1024,128]{1,0:T(8,128)} %get-tuple-element.6.ai_ref, s32[128,128]{1,0:T(8,128)} %pad.4.slots_t_ref), custom_call_target="tpu_custom_call" | custom-call | tf_op jit(solution)/shard_map/pick/pallas_call | solution.py:297
  87.3 1.5 %copy.19 = f32[2,50,128]{2,0,1:T(2,128)} copy(f32[2,50,128]{2,1,0:T(8,128)} %pick.1) | data formatting | bytes 102400
  88.7 0.0 copy-done.1
  88.7 0.6 copy.23
  (2 shorter events, 0.0 us)
Async XLA Ops:
  5.2 1.3 %copy-start = (bf16[128,32,64]{0,1,2:T(8,128)(2,1)}, bf16[128,32,64]{0,1,2:T(8,128)(2,1)S(1)}, u32[]{:S(2)}) copy-start(bf16[128,32,64]{0,1,2:T(8,128)(2,1)S(1)} %copy.21) | copy-start | bytes 1572868
  83.6 5.1 %copy-start.1 = (f32[32,128]{1,0:T(8,128)S(1)}, f32[32,128]{1,0:T(8,128)}, u32[]{:S(2)}) copy-start(f32[32,128]{1,0:T(8,128)} %get-tuple-element.19) | copy-start | bytes 49156

commit v4 on v3

--- a/solution.py
+++ b/solution.py
@@ -29,8 +29,8 @@
 
 
 def main_kernel(
-    own_ref, mine_ref, slots_ref, initial_ref, ar_ref, ai_ref, out_ref,
-    blocks, oper_ref, degree_ref, land, image, part_gram, land_rep, land_grp,
+    own_ref, mine_ref, slots_ref, slots_t_ref, initial_ref, align_ref, out_ref,
+    ratio, found, blocks, oper_ref, degree_ref, land, image, part_gram, land_rep, land_grp,
     copy_sem, ring_send, ring_recv, send, recv, send_rep, recv_rep, send_grp, recv_grp,
 ):
     groups, replicas = lax.axis_size("grp"), lax.axis_size("rep")
@@ -97,6 +97,7 @@
         hop(mine_ref, replicas - 1, part, left_rep).start()
 
     to_first.wait()
+    found[...] = jnp.zeros_like(found)
     degree_ref[...] = jnp.full(degree_ref.shape, EPS, jnp.float32)
 
     def block_step(turn, _):
@@ -157,14 +158,23 @@
             oper_ref[here, own:] = count * moment_im
             degree_ref[...] += jnp.sum(count * energy, axis=0, keepdims=True)
             scale = 1.0 / (energy + EPS)
-            ar_ref[here, :] = moment_re * scale
-            ai_ref[here, :] = moment_im * scale
+            local = pl.ds(pl.multiple_of(part * half, half), half)
+            ratio[0, local] = moment_re * scale
+            ratio[1, local] = moment_im * scale
             return 0
 
         lax.fori_loop(0, 2, tile, 0)
+        names = slots_t_ref[...]
+        here = names // particles == owner
+        lane = names % particles
+        for side in range(2):
+            got = jnp.take_along_axis(ratio[side].T, lane, axis=1, mode="promise_in_bounds")
+            found[side] = jnp.where(here, got, found[side])
         return 0
 
     lax.fori_loop(0, replicas, block_step, 0)
+    for side in range(2):
+        align_ref[side] = found[side].T[:slots]
 
     started = []
     for turn in range(ITERS):
@@ -228,25 +238,6 @@
         hop(mine_ref, middle, part, right_rep).wait_send()
 
 
-def pick_kernel(ar_ref, ai_ref, slots_t_ref, align_ref):
-    slots, wide = align_ref.shape[1:]
-    names = slots_t_ref[...]
-    lane = names % wide
-    owner = names // wide
-
-    def pick(block, found):
-        rows = pl.ds(pl.multiple_of(block * wide, wide), wide)
-        here = owner == block
-        got_re = jnp.take_along_axis(ar_ref[rows, :].T, lane, axis=1, mode="promise_in_bounds")
-        got_im = jnp.take_along_axis(ai_ref[rows, :].T, lane, axis=1, mode="promise_in_bounds")
-        return (jnp.where(here, got_re, found[0]), jnp.where(here, got_im, found[1]))
-
-    zero = jnp.zeros(names.shape, jnp.float32)
-    found = lax.fori_loop(0, ar_ref.shape[0] // wide, pick, (zero, zero))
-    align_ref[0] = found[0].T[:slots]
-    align_ref[1] = found[1].T[:slots]
-
-
 def shards(coefficients, truncation, neighbours, initial):
     groups = lax.axis_size("grp")
     replicas = lax.axis_size("rep")
@@ -266,13 +257,17 @@
     rows = initial.shape[0]
     order = rows // 2
     dma = pltpu.SemaphoreType.DMA
-    table = jax.ShapeDtypeStruct((group, particles), jnp.float32)
-    ratio_re, ratio_im, vectors = pl.pallas_call(
+    alignment, vectors = pl.pallas_call(
         main_kernel,
-        out_shape=[table, table, jax.ShapeDtypeStruct(initial.shape, jnp.float32)],
-        in_specs=[VMEM] * 4,
-        out_specs=[VMEM] * 3,
+        out_shape=[
+            jax.ShapeDtypeStruct((2, slots, particles), jnp.float32),
+            jax.ShapeDtypeStruct(initial.shape, jnp.float32),
+        ],
+        in_specs=[VMEM] * 5,
+        out_specs=[VMEM] * 2,
         scratch_shapes=[
+            pltpu.VMEM((2, particles, particles), jnp.float32),
+            pltpu.VMEM((2,) + padded.shape, jnp.float32),
             pltpu.VMEM((replicas,) + mine.shape, mine.dtype),
             pltpu.VMEM((group, 2 * particles), jnp.float32),
             pltpu.VMEM((1, particles), jnp.float32),
@@ -293,14 +288,7 @@
         ],
         compiler_params=pltpu.CompilerParams(collective_id=0, has_side_effects=True),
         name="main",
-    )(own, mine, in_group, initial)
-    alignment = pl.pallas_call(
-        pick_kernel,
-        out_shape=jax.ShapeDtypeStruct((2, slots, particles), jnp.float32),
-        in_specs=[VMEM] * 3,
-        out_specs=VMEM,
-        name="pick",
-    )(ratio_re, ratio_im, padded)
+    )(own, mine, in_group, padded, initial)
     return alignment, vectors
 
 

time: 89.7 us -> 86.1 us (0.960)
  Pallas kernels: 80.7 us -> 77.6 us
    pallas_call x2 -> x1, Pallas kernels: 80.7 us -> 77.6 us  [shards(): pl.pallas_call(main_kernel, out_shape=[jax.ShapeDtypeStruct((2, slots, pa...]
    pallas_call x0 -> x1, local copies, waits for them, and re-layouts: none -> 1.47 us  [shards(): pl.pallas_call(main_kernel, out_shape=[jax.ShapeDtypeStruct((2, slots, pa...]
    unnamed x8 -> x9, local copies, waits for them, and re-layouts: 4.23 us -> 2.97 us
where the time goes in v4:
time: 86.1 us; the launch traced here: 85.8 us
  Pallas kernels  77.6 us (90%)
  local copies, waits for them, and re-layouts  6.1 us (7%)
  other arithmetic  1.39 us (2%)
    pallas_call x1, Pallas kernels, shards(): pl.pallas_call(main_kernel, out_shape=[jax.ShapeDtypeStruct((2, slots, pa...  77.6 us
    unnamed x9, local copies, waits for them, and re-layouts  2.97 us

profile of v4, /device:TPU:0, one launch (start us, length us, event | category | flops | bytes accessed | tf_op | source)
XLA Modules:
  0.0 85.8 jit_solution(10288472311863964825)
XLA Ops:
  0.6 1.3 %copy.14 = bf16[128,2048]{0,1:T(8,128)(2,1)S(1)} copy(bf16[128,2048]{1,0:T(8,128)(2,1)} %param.4) | data formatting | bytes 1048576 | tf_op args[0]
  1.9 0.0 copy-start.2
  2.0 0.3 copy.21
  2.3 0.0 copy-start
  2.3 0.1 fusion
  2.4 0.2 copy-done.2
  2.6 0.1 pad_add_fusion
  2.7 0.0 copy-start.1
  2.7 1.2 %maximum_select_fusion.own_ref = bf16[64,32,256]{2,1,0:T(8,128)(2,1)} fusion(bf16[64,16,128]{2,1,0:T(8,128)(2,1)S(1)} %get-tuple-element.9, bf16[64,16,128]{2,1,0:T(8,128)(2,1)S(1)} %get-tuple-element.8, bf16[64,32,128]{2,1,0:T(8,128)(2,1)S(1)} %bitcast.7, pred[64,32]{1,0:T(8,128)(4,1)S(1)} %pad_add_fusion), kind=kLoop, calls=%fused_computation | loop fusion | flops 3670016 | bytes 2099200 | tf_op jit(solution)/shard_map/jit(_where)/select_n | solution.py:254
  3.9 0.0 copy-done
  3.9 0.0 copy-done.1
  3.9 0.1 copy.16
  4.1 0.6 pad.4.slots_t_ref
  4.7 0.7 copy.18.slots_ref
  5.4 77.6 %main.1 = (f32[2,50,128]{2,1,0:T(8,128)}, f32[32,128]{1,0:T(8,128)}) custom-call(bf16[64,32,256]{2,1,0:T(8,128)(2,1)} %maximum_select_fusion.own_ref, bf16[64,32,128]{2,1,0:T(8,128)(2,1)} %bitcast.8, s32[50,128]{1,0:T(8,128)} %copy.18.slots_ref, s32[128,128]{1,0:T(8,128)} %pad.4.slots_t_ref, f32[32,128]{1,0:T(8,128)} %initial_ref.1), custom_call_target="tpu_custom_call" | custom-call | tf_op jit(solution)/shard_map/main/pallas_call | solution.py:260
  83.0 1.5 %copy.19 = f32[2,50,128]{2,0,1:T(2,128)} copy(f32[2,50,128]{2,1,0:T(8,128)} %get-tuple-element.6) | data formatting | bytes 102400 | tf_op jit(solution)/shard_map/main/pallas_call | solution.py:260
  84.5 1.3 %copy.23 = f32[32,128]{1,0:T(8,128)} copy(f32[32,128]{1,0:T(8,128)} %get-tuple-element.13) | data formatting | bytes 32768
  (3 shorter events, 0.0 us)
Async XLA Ops:
  1.9 0.7 copy-start.2
  2.3 1.6 %copy-start = (bf16[128,32,64]{0,1,2:T(8,128)(2,1)}, bf16[128,32,64]{0,1,2:T(8,128)(2,1)S(1)}, u32[]{:S(2)}) copy-start(bf16[128,32,64]{0,1,2:T(8,128)(2,1)S(1)} %copy.21) | copy-start | bytes 1572868
  2.7 1.2 %copy-start.1 = (s32[50,128]{1,0:T(8,128)S(1)}, s32[50,128]{1,0:T(8,128)}, u32[]{:S(2)}) copy-start(s32[50,128]{1,0:T(8,128)} %param.6) | copy-start | bytes 76804
